TPU v7x, 32 devices: a whole 2x2x4 slice. The times are simulated.
32 devices in a mesh: tok: 4 (over y, x), hid: 2 (over core), voc: 4 (over z).
Axes of the slice: x: 2, y: 2, z: 4, core: 2. Of those that a mesh axis runs over, the one named last changes fastest.
Arguments:
- student_hidden: bfloat16 [512, 8192], P('tok', ('hid', 'voc')), may hold values from -8 to 8
- teacher_hidden: bfloat16 [512, 16384], P('tok', ('hid', 'voc')), may hold values from -8 to 8
- student_head: bfloat16 [8192, 2048], P('hid', 'voc'), may hold values from -2 to 2
- teacher_head: bfloat16 [16384, 2048], P('hid', 'voc'), may hold values from -2 to 2
- loss_weight: float32 [512], P('tok'), may hold values from 128 to 1024
Outputs:
- grad_hidden: bfloat16 [512, 8192], P('tok', ('hid', 'voc'))
- mean_loss: float32 [], replicated
All inputs are finite; a program needn't handle non-finite values.
Results may differ from a plain program's by a relative error of at most 0.001.
The roundings to bfloat16 on the way count: a program that leaves them out, or rounds other values in their place, can miss the bound.
Values may be sent and summed in bfloat16 or wider, within the bound.
A program may use at most 64 MiB of HBM per device.

v0:
```python
import jax
import jax.numpy as jnp
from jax import lax
from jax.sharding import PartitionSpec as P


def divergence_terms(student_logits, teacher_logits, weights):
    differences = teacher_logits - student_logits
    peak_student, peak_teacher = lax.pmax(
        (jnp.max(student_logits, axis=1), jnp.max(teacher_logits, axis=1)), "voc"
    )
    scaled_student = jnp.exp(student_logits - peak_student[:, None])
    scaled_teacher = jnp.exp(teacher_logits - peak_teacher[:, None])
    total_student, total_teacher, cross_sum = lax.psum(
        (
            jnp.sum(scaled_student, axis=1),
            jnp.sum(scaled_teacher, axis=1),
            jnp.sum(scaled_teacher * differences, axis=1),
        ),
        "voc",
    )
    student_lse = peak_student + jnp.log(total_student)
    teacher_lse = peak_teacher + jnp.log(total_teacher)
    divergence = cross_sum / total_teacher - teacher_lse + student_lse
    prob_gap = jnp.exp(student_logits - student_lse[:, None]) - jnp.exp(
        teacher_logits - teacher_lse[:, None]
    )
    scaled_gap = (weights[:, None] * prob_gap).astype(jnp.bfloat16)
    return (divergence, scaled_gap)


def shards(student_hidden, teacher_hidden, student_head, teacher_head, loss_weight):
    student_block, teacher_block = (
        lax.all_gather(student_hidden, "voc", axis=1, tiled=True),
        lax.all_gather(teacher_hidden, "voc", axis=1, tiled=True),
    )
    vocab_local = student_head.shape[1]
    row_count = student_block.shape[0] // lax.axis_size("hid")
    joined = lax.psum_scatter(
        jnp.concatenate(
            [
                jnp.dot(student_block, student_head, preferred_element_type=jnp.float32),
                jnp.dot(teacher_block, teacher_head, preferred_element_type=jnp.float32),
            ],
            axis=1,
        ),
        "hid",
        scatter_dimension=0,
        tiled=True,
    )
    student_logits = joined[:, :vocab_local]
    teacher_logits = joined[:, vocab_local:]
    weights = lax.dynamic_slice_in_dim(loss_weight, lax.axis_index("hid") * row_count, row_count)
    divergence, scaled_gap = divergence_terms(student_logits, teacher_logits, weights)
    token_total = loss_weight.shape[0] * lax.axis_size("tok")
    loss_total = lax.psum(jnp.sum(divergence), ("tok", "hid"))
    grad_terms = lax.dot_general(
        lax.all_gather(scaled_gap, "hid", axis=0, tiled=True),
        student_head,
        (((1,), (1,)), ((), ())),
        preferred_element_type=jnp.float32,
    )
    grad_hidden = lax.psum_scatter(grad_terms, "voc", scatter_dimension=1, tiled=True).astype(
        jnp.bfloat16
    )
    mean_loss = loss_total / token_total
    return (grad_hidden, mean_loss)


def solution(mesh):
    placed = (
        P("tok", ("hid", "voc")),
        P("tok", ("hid", "voc")),
        P("hid", "voc"),
        P("hid", "voc"),
        P("tok"),
    )
    return jax.shard_map(
        shards,
        mesh=mesh,
        in_specs=placed,
        out_specs=(P("tok", ("hid", "voc")), P()),
        check_vma=False,
    )
```

profile of v0, /device:TPU:1, one launch (start us, length us, event | category | flops | bytes accessed | tf_op | source)
XLA Modules:
  0.0 182.9 jit_solution(341071947678527449)
XLA Ops:
  7.2 0.0 all-gather.3.cloned.1.call-start
  7.2 0.7 all-gather.3.cloned.1.call-update
  7.9 0.0 all-gather.5.cloned.1.call-start
  7.9 0.7 all-gather.5.cloned.1.call-update
  8.6 0.0 reduce-scatter.3.cloned.1.call-start
  8.7 30.5 %all-gather.3.cloned.1.call-done = bf16[128,4096]{1,0:T(8,128)(2,1)} async-done(((bf16[128,1024]{1,0:T(8,128)(2,1)}), bf16[128,4096]{1,0:T(8,128)(2,1)}) %all-gather.3.cloned.1.call-update) | async-done | bytes 1048592 | tf_op jit(solution)/shard_map/all_gather | solution.py:34
  39.1 3.2 %fusion.1 = f32[128,512]{1,0:T(8,128)S(1)} fusion(bf16[128,4096]{1,0:T(8,128)(2,1)} %all-gather.3.cloned.1.call-done, bf16[4096,512]{1,0:T(8,128)(2,1)} %param.7), kind=kOutput, calls=%fused_computation.11 | convolution fusion | flops 536870912 | bytes 5505024 | tf_op jit(solution)/shard_map/dot_general | solution.py:42
  42.4 0.0 copy-start
  42.4 43.7 %all-gather.5.cloned.1.call-done = bf16[128,8192]{1,0:T(8,128)(2,1)} async-done(((bf16[128,2048]{1,0:T(8,128)(2,1)}), bf16[128,8192]{1,0:T(8,128)(2,1)}) %all-gather.5.cloned.1.call-update) | async-done | bytes 2097168 | tf_op jit(solution)/shard_map/all_gather | solution.py:35
  86.1 5.3 %fusion.2 = f32[128,512]{1,0:T(8,128)S(1)} fusion(bf16[128,8192]{1,0:T(8,128)(2,1)} %all-gather.5.cloned.1.call-done, bf16[8192,512]{1,0:T(8,128)(2,1)} %param.8), kind=kOutput, calls=%fused_computation.12 | convolution fusion | flops 1073741824 | bytes 10747904 | tf_op jit(solution)/shard_map/dot_general | solution.py:43
  91.4 0.8 pad_maximum_fusion
  92.2 0.0 reduce-scatter.3.cloned.1.call-update
  92.2 0.0 reduce-scatter.5.cloned.1.call-start
  92.3 0.0 copy-done
  92.3 0.1 dynamic_slice.3
  92.4 7.3 %reduce-scatter.3.cloned.1.call-done = f32[64,1024]{1,0:T(8,128)} async-done(((f32[128,1024]{1,0:T(8,128)}), f32[64,1024]{1,0:T(8,128)}) %reduce-scatter.3.cloned.1.call-update) | async-done | bytes 262160 | tf_op jit(solution)/shard_map/reduce_scatter | solution.py:39
  99.6 1.1 slice_reduce_fusion.1
  100.7 10.1 %all-reduce.1 = (f32[64]{0:T(128)S(1)}, f32[64]{0:T(128)S(1)}) all-reduce(f32[64]{0:T(128)S(1)} %get-tuple-element.6, f32[64]{0:T(128)S(1)} %get-tuple-element.5), channel_id=1, replica_groups=mesh['tok'=4,'hid'=2,'voc'=4] {'voc'}, use_global_device_ids=true, to_apply=%region_6.0 | all-reduce | flops 128 | bytes 1024 | tf_op jit(solution)/shard_map/pmax | solution.py:9
  110.8 1.2 multiply_reduce_fusion
  112.0 6.6 %all-reduce = (f32[64]{0:T(128)S(1)}, f32[64]{0:T(128)S(1)}, f32[64]{0:T(128)S(1)}) all-reduce(f32[64]{0:T(128)S(1)} %get-tuple-element.3, f32[64]{0:T(128)S(1)} %get-tuple-element.4, f32[64]{0:T(128)S(1)} %get-tuple-element.2), channel_id=1, replica_groups=mesh['tok'=4,'hid'=2,'voc'=4] {'voc'}, use_global_device_ids=true, to_apply=%region_8.0 | all-reduce | flops 192 | bytes 1536 | tf_op jit(solution)/shard_map/psum | solution.py:14
  118.6 0.6 add_reduce_fusion
  119.2 1.1 multiply_convert_fusion
  120.3 5.4 %all_gather.11 = bf16[128,512]{1,0:T(8,128)(2,1)S(1)} all-gather(bf16[64,512]{1,0:T(8,128)(2,1)S(1)} %multiply_convert_fusion), channel_id=1, replica_groups=mesh['tok'=4,'hid'=2,'voc'=4] {'hid'}, dimensions={0}, use_global_device_ids=true | all-gather | bytes 196608 | tf_op jit(solution)/shard_map/all_gather | solution.py:58
  125.8 5.0 %fusion.3 = f32[128,4096]{1,0:T(8,128)} fusion(bf16[128,512]{1,0:T(8,128)(2,1)S(1)} %all_gather.11, bf16[4096,512]{1,0:T(8,128)(2,1)} %param.7), kind=kOutput, calls=%fused_computation.13 | convolution fusion | flops 536870912 | bytes 6422528 | tf_op jit(solution)/shard_map/dot_general | solution.py:57
  130.8 0.0 reduce-scatter.5.cloned.1.call-update
  130.8 12.1 %psum.31 = f32[]{:T(128)} all-reduce(f32[]{:T(128)} %get-tuple-element.12), channel_id=1, replica_groups=mesh['tok'=4,'hid'=2,'voc'=4] {'tok','hid'}, use_global_device_ids=true, to_apply=%region_13.0 | all-reduce | flops 1 | bytes 8 | tf_op jit(solution)/shard_map/psum | solution.py:56
  143.6 29.9 %reduce-scatter.5.cloned.1.call-done = f32[128,1024]{1,0:T(8,128)} async-done(((f32[128,4096]{1,0:T(8,128)}), f32[128,1024]{1,0:T(8,128)}) %reduce-scatter.5.cloned.1.call-update) | async-done | bytes 524304 | tf_op jit(solution)/shard_map/reduce_scatter | solution.py:63
  173.5 1.8 convert_element_type.7
Async XLA Ops:
  7.2 32.0 %all-gather.3.cloned.1.call-start = ((), (), s32[]{:S(2)}) async-start(), calls=%async_computation.2 | async-start | bytes 1310720 | tf_op jit(solution)/shard_map/all_gather | solution.py:34
  7.9 78.2 %all-gather.5.cloned.1.call-start = ((), (), s32[]{:S(2)}) async-start(), calls=%async_computation.3 | async-start | bytes 2621440 | tf_op jit(solution)/shard_map/all_gather | solution.py:35
  8.6 91.0 %reduce-scatter.3.cloned.1.call-start = ((), (), s32[]{:S(2)}) async-start(), calls=%async_computation.4 | async-start | bytes 786432 | tf_op jit(solution)/shard_map/reduce_scatter | solution.py:39
  42.4 49.9 %copy-start = (f32[128]{0:T(128)S(1)}, f32[128]{0:T(128)}, u32[]{:S(2)}) copy-start(f32[128]{0:T(128)} %param.9) | copy-start | bytes 1540
  92.2 81.3 %reduce-scatter.5.cloned.1.call-start = ((), (), s32[]{:S(2)}) async-start(), calls=%async_computation.5 | async-start | bytes 2621440 | tf_op jit(solution)/shard_map/reduce_scatter | solution.py:63
Sparse Core Ops, SparseCore 0:
  9.5 29.5 all-gather.2
  40.7 45.3 all-gather.4
  92.3 7.2 reduce-scatter.2
  130.9 42.5 reduce-scatter.4
where the time goes:
time: 184 us; the launch traced here: 183 us
  waiting for transfers between devices  113 us (61%)
  blocking collectives  34.3 us (19%)
  between operations  15.6 us (8%)
  matrix products  13.5 us (7%)
  other arithmetic  6.6 us (4%)
    all_gather x1, waiting for transfers between devices, shards(): lax.all_gather(teacher_hidden, 'voc', axis=1, tiled=True)  43.7 us
    all_gather x1, waiting for transfers between devices, shards(): lax.all_gather(student_hidden, 'voc', axis=1, tiled=True)  30.5 us
    reduce_scatter x1, waiting for transfers between devices, shards(): lax.psum_scatter(grad_terms, 'voc', scatter_dimension=1, tiled=True)  29.9 us
    psum x1, blocking collectives, shards(): loss_total = lax.psum(jnp.sum(divergence), ('tok', 'hid'))  12.1 us
    pmax x1, blocking collectives, divergence_terms(): lax.pmax((jnp.max(student_logits, axis=1), jnp.max(teacher_logits, axis=1...  10.1 us
    reduce_scatter x1, waiting for transfers between devices, shards(): lax.psum_scatter(jnp.concatenate([jnp.dot(student_block, student_head, pr...  7.27 us
    psum x1, blocking collectives, divergence_terms(): lax.psum((jnp.sum(scaled_student, axis=1), jnp.sum(scaled_teacher, axis=1...  6.63 us
    all_gather x1, blocking collectives, shards(): lax.all_gather(scaled_gap, 'hid', axis=0, tiled=True)  5.44 us
  transfers between devices with their start and end apart: 4, of which 4 were waited for; matrix products, arithmetic and copies ran while one was open for 2% of the time, Pallas kernels for 0%

commit v1 on v0

--- a/solution.py
+++ b/solution.py
@@ -1,7 +1,352 @@
+import functools
+
 import jax
 import jax.numpy as jnp
 from jax import lax
+from jax.experimental import pallas as pl
+from jax.experimental.pallas import tpu as pltpu
 from jax.sharding import PartitionSpec as P
+
+MESH = pl.DeviceIdType.MESH
+F32 = jnp.float32
+BF16 = jnp.bfloat16
+
+
+def fused(n, nt, x_ref, y_ref, w_ref, sw_hbm, tw_hbm, out, loss_out,
+          wf, tw, tg, sp, spx, ssum, srr, tacc, tpx, stat, gap, wcol, lossb, acc,
+          lc, wz_s, wz_r, wt_s, wt_r, th_s, th_r, px_s, px_r, rs_s, rs_r,
+          st_s, st_r, gz_s, gz_r, gx_s, gx_r, ls_s, ls_r):
+    z = lax.axis_index("voc")
+    t = lax.axis_index("tok")
+    h = lax.axis_index("hid")
+    rows, ks = x_ref.shape
+    kt = y_ref.shape[1]
+    half = rows // 2
+    quarter = ks // nt
+    partner = {"hid": 1 - h}
+    mine = pl.ds(pl.multiple_of(h * half, half), half)
+    theirs = pl.ds(pl.multiple_of((1 - h) * half, half), half)
+    me = t * 2 + h
+
+    def rc(src, dst, ss, rs, dev):
+        return pltpu.make_async_remote_copy(
+            src_ref=src, dst_ref=dst, send_sem=ss, recv_sem=rs,
+            device_id=dev, device_id_type=MESH)
+
+    def zdev(k):
+        return lax.rem(z + k, n)
+
+    plane = []
+    for q in range(nt):
+        for c in range(2):
+            if q or c:
+                plane.append((lax.rem(t + q, nt), lax.rem(h + c, 2)))
+
+    own_w = pltpu.make_async_copy(sw_hbm.at[pl.ds(pl.multiple_of(z * ks, ks), ks)], wf.at[z], lc.at[n])
+    own_w.start()
+
+    def tw_copy(i):
+        return pltpu.make_async_copy(tw_hbm.at[pl.ds(pl.multiple_of(i * kt, kt), kt)], tw.at[i], lc.at[i])
+
+    barrier = pltpu.get_barrier_semaphore()
+    for k in range(1, n):
+        pl.semaphore_signal(barrier, inc=1, device_id={"voc": zdev(k)}, device_id_type=MESH)
+    for (a, b) in plane:
+        pl.semaphore_signal(barrier, inc=1, device_id={"tok": a, "hid": b}, device_id_type=MESH)
+    pl.semaphore_wait(barrier, n - 1 + len(plane))
+
+    def part(i):
+        return pl.ds(pl.multiple_of(i * quarter, quarter), quarter)
+
+    def wz(j):
+        return rc(sw_hbm.at[pl.ds(pl.multiple_of(j * ks + t * quarter, quarter), quarter)],
+                  wf.at[z, part(t)], wz_s.at[j], wz_r.at[z], {"voc": j})
+
+    def wz_in(j):
+        return rc(wf.at[j, part(t)], wf.at[j, part(t)], wz_s.at[j], wz_r.at[j], {"voc": j})
+
+    def wt(j, dst_t):
+        return rc(wf.at[j, part(t)], wf.at[j, part(t)], wt_s.at[j, dst_t], wt_r.at[j, t], {"tok": dst_t})
+
+    def wt_in(j, src_t):
+        return rc(wf.at[j, part(src_t)], wf.at[j, part(src_t)], wt_s.at[j, src_t], wt_r.at[j, src_t], {"tok": src_t})
+
+    def sides(d):
+        return ((z - d, z - d >= 0), (z + d, z + d < n))
+
+    for d in range(1, n):
+        for j, ok in sides(d):
+            @pl.when(ok)
+            def _(j=j):
+                wz(j).start()
+
+    def piece(r):
+        return pl.ds(r * half, half)
+
+    def own_y(r, side):
+        return rc(y_ref.at[piece(r)], tg.at[z, piece(r)], th_s.at[side, z, r], th_r.at[z, r],
+                  {"voc": z + (1 if side else -1)})
+
+    def relay_y(i, r, side):
+        return rc(tg.at[i, piece(r)], tg.at[i, piece(r)], th_s.at[side, i, r], th_r.at[i, r],
+                  {"voc": z + (1 if side else -1)})
+
+    room = (z - 1 >= 0, z + 1 < n)
+    for r in range(2):
+        for side in range(2):
+            @pl.when(room[side])
+            def _(r=r, side=side):
+                own_y(r, side).start()
+
+    for k in range(n):
+        tw_copy(zdev(k)).start()
+
+    wcol[...] = jnp.transpose(jnp.broadcast_to(w_ref[...], (rows, rows)))
+
+    for d in range(1, n):
+        for j, ok in sides(d):
+            @pl.when(ok)
+            def _(j=j):
+                wz_in(j).wait_recv()
+                for q in range(1, nt):
+                    wt(j, lax.rem(t + q, nt)).start()
+
+    def teacher_dot(src, i, first):
+        tw_copy(i).wait()
+        step = kt // 2
+
+        @pl.loop(0, 2)
+        def _(s):
+            cols = pl.ds(pl.multiple_of(s * step, step), step)
+            term = jnp.dot(src[:, cols], tw[i, cols, :], preferred_element_type=F32)
+            if first:
+                @pl.when(s == 0)
+                def _():
+                    tacc[...] = term
+
+                @pl.when(s > 0)
+                def _():
+                    tacc[...] += term
+            else:
+                tacc[...] += term
+
+    teacher_dot(y_ref, z, True)
+
+    def take_y(d, dot):
+        for r in range(2):
+            for side, (i, ok) in enumerate(sides(d)):
+                @pl.when(ok)
+                def _(i=i, side=side, r=r):
+                    relay_y(i, r, side).wait_recv()
+                    if d < n - 1:
+                        on = 1 - side
+
+                        @pl.when(room[on])
+                        def _():
+                            relay_y(i, r, on).start()
+        if dot:
+            dot_y(d)
+
+    def dot_y(d):
+        for i, ok in sides(d):
+            @pl.when(ok)
+            def _(i=i):
+                teacher_dot(tg.at[i], i, False)
+
+    def student(k):
+        j = zdev(k)
+        if k == 0:
+            own_w.wait()
+        else:
+            for q in range(1, nt):
+                wt_in(j, lax.rem(t + q, nt)).wait_recv()
+        sp[j] = jnp.dot(x_ref[...], wf[j], preferred_element_type=F32)
+        rc(sp.at[j, theirs], spx.at[j], px_s.at[j], px_r.at[j], partner).start()
+
+    def student_send(k):
+        j = zdev(k)
+        rc(sp.at[j, theirs], spx.at[j], px_s.at[j], px_r.at[j], partner).wait_recv()
+        ssum[j] = sp[j, mine, :] + spx[j]
+        if k:
+            rc(ssum.at[j], srr.at[z], rs_s.at[j], rs_r.at[z], {"voc": j}).start()
+
+    student(0)
+    for d in range(1, n - 1):
+        take_y(d, True)
+    student_send(0)
+    for k in range(1, n):
+        student(k)
+        student_send(k)
+    take_y(n - 1, True)
+
+    tx = rc(tacc.at[theirs], tpx, px_s.at[n], px_r.at[n], partner)
+    tx.start()
+    sl = ssum[z]
+    for k in range(1, n):
+        j = zdev(k)
+        rc(srr.at[j], srr.at[j], rs_s.at[j], rs_r.at[j], {"voc": j}).wait_recv()
+        sl = sl + srr[j]
+    ssum[z] = sl
+    ms = jnp.max(sl, axis=1, keepdims=True)
+    ss = jnp.sum(jnp.exp(sl - ms), axis=1, keepdims=True)
+    tx.wait_recv()
+    tl = tacc[mine, :] + tpx[...]
+    tpx[...] = tl
+    mt = jnp.max(tl, axis=1, keepdims=True)
+    et = jnp.exp(tl - mt)
+    st = jnp.sum(et, axis=1, keepdims=True)
+    cr = jnp.sum(et * (tl - sl), axis=1, keepdims=True)
+    lane = lax.broadcasted_iota(jnp.int32, (half, 128), 1)
+    stat[z] = jnp.where(lane == 0, ms, jnp.where(lane == 1, mt, jnp.where(
+        lane == 2, ss, jnp.where(lane == 3, st, cr))))
+
+    def stx(j, src):
+        return rc(stat.at[src], stat.at[src], st_s.at[j], st_r.at[src], {"voc": j})
+
+    for k in range(1, n):
+        stx(zdev(k), z).start()
+    for k in range(1, n):
+        stx(zdev(k), zdev(k)).wait_recv()
+    parts = [stat[j] for j in range(n)]
+    top = parts[0]
+    for p in parts[1:]:
+        top = jnp.maximum(top, p)
+    big_s, big_t = top[:, 0:1], top[:, 1:2]
+    tot_s = jnp.zeros_like(big_s)
+    tot_t = jnp.zeros_like(big_s)
+    cross = jnp.zeros_like(big_s)
+    for p in parts:
+        es = jnp.exp(p[:, 0:1] - big_s)
+        ets = jnp.exp(p[:, 1:2] - big_t)
+        tot_s = tot_s + p[:, 2:3] * es
+        tot_t = tot_t + p[:, 3:4] * ets
+        cross = cross + p[:, 4:5] * ets
+    lse_s = big_s + jnp.log(tot_s)
+    lse_t = big_t + jnp.log(tot_t)
+    scale = wcol[mine, :][:, 0:1]
+    gap[z, mine, :] = (scale * (jnp.exp(ssum[z] - lse_s) - jnp.exp(tpx[...] - lse_t))).astype(BF16)
+
+    def gz(j, src):
+        return rc(gap.at[src, mine], gap.at[src, mine], gz_s.at[j], gz_r.at[src], {"voc": j})
+
+    def gx(src, side):
+        return rc(gap.at[src, side], gap.at[src, side], gx_s.at[src], gx_r.at[src], partner)
+
+    for d in range(1, n):
+        for j, ok in sides(d):
+            @pl.when(ok)
+            def _(j=j):
+                gz(j, z).start()
+    gx(z, mine).start()
+
+    div = cross / tot_t - lse_t + lse_s
+    lossb[me] = jnp.broadcast_to(jnp.sum(div, axis=0, keepdims=True), (8, 128))
+
+    def ls(a, b, src):
+        return rc(lossb.at[src], lossb.at[src], ls_s.at[a * 2 + b], ls_r.at[src], {"tok": a, "hid": b})
+
+    for (a, b) in plane:
+        ls(a, b, me).start()
+
+    def grad_dot(j, first):
+        term = lax.dot_general(gap[j], wf[j], (((1,), (1,)), ((), ())), preferred_element_type=F32)
+        if first:
+            acc[...] = term
+        else:
+            acc[...] += term
+
+    gx(z, theirs).wait_recv()
+    grad_dot(z, True)
+    for d in range(1, n):
+        for j, ok in sides(d):
+            @pl.when(ok)
+            def _(j=j):
+                gz(j, j).wait_recv()
+                gx(j, mine).start()
+    for k in range(1, n):
+        j = zdev(k)
+        gx(j, theirs).wait_recv()
+        grad_dot(j, False)
+    out[...] = acc[...].astype(BF16)
+
+    for (a, b) in plane:
+        ls(a, b, a * 2 + b).wait_recv()
+    total = lossb[0]
+    for p in range(1, nt * 2):
+        total = total + lossb[p]
+    loss_out[0, 0] = total[0, 0] / (rows * nt)
+
+    for k in range(1, n):
+        j = zdev(k)
+        wz(j).wait_send()
+        for q in range(1, nt):
+            wt(j, lax.rem(t + q, nt)).wait_send()
+        rc(ssum.at[j], srr.at[z], rs_s.at[j], rs_r.at[z], {"voc": j}).wait_send()
+        stx(j, z).wait_send()
+        gz(j, z).wait_send()
+    for r in range(2):
+        for side in range(2):
+            @pl.when(room[side])
+            def _(r=r, side=side):
+                own_y(r, side).wait_send()
+    for d in range(1, n - 1):
+        for r in range(2):
+            for side, (i, ok) in enumerate(sides(d)):
+                on = 1 - side
+
+                @pl.when(jnp.logical_and(ok, room[on]))
+                def _(i=i, r=r, on=on):
+                    relay_y(i, r, on).wait_send()
+    for k in range(n):
+        j = zdev(k)
+        rc(sp.at[j, theirs], spx.at[j], px_s.at[j], px_r.at[j], partner).wait_send()
+        gx(j, mine).wait_send()
+    tx.wait_send()
+    for (a, b) in plane:
+        ls(a, b, me).wait_send()
+
+
+def fused_shards(n, nt, student_hidden, teacher_hidden, student_head, teacher_head, loss_weight):
+    rows, ks = student_hidden.shape
+    kt = teacher_hidden.shape[1]
+    v = student_head.shape[1]
+    half = rows // 2
+    dma = lambda *s: pltpu.SemaphoreType.DMA(s)
+    vmem = lambda s, d: pltpu.VMEM(s, d)
+    whole = pl.BlockSpec(memory_space=pltpu.VMEM)
+    anywhere = pl.BlockSpec(memory_space=pl.ANY)
+    grad, loss = pl.pallas_call(
+        functools.partial(fused, n, nt),
+        out_shape=(jax.ShapeDtypeStruct((rows, ks), BF16), jax.ShapeDtypeStruct((1, 1), F32)),
+        in_specs=[whole, whole, whole, anywhere, anywhere],
+        out_specs=(whole, pl.BlockSpec(memory_space=pltpu.SMEM)),
+        scratch_shapes=[
+            vmem((n, ks, v), BF16),
+            vmem((n, kt, v), BF16),
+            vmem((n, rows, kt), BF16),
+            vmem((n, rows, v), F32),
+            vmem((n, half, v), F32),
+            vmem((n, half, v), F32),
+            vmem((n, half, v), F32),
+            vmem((rows, v), F32),
+            vmem((half, v), F32),
+            vmem((n, half, 128), F32),
+            vmem((n, rows, v), BF16),
+            vmem((rows, rows), F32),
+            vmem((nt * 2, 8, 128), F32),
+            vmem((rows, ks), F32),
+            dma(n + 1),
+            dma(n), dma(n), dma(n, nt), dma(n, nt),
+            dma(2, n, 2), dma(n, 2),
+            dma(n + 1), dma(n + 1), dma(n), dma(n),
+            dma(n), dma(n), dma(n), dma(n), dma(n), dma(n),
+            dma(nt * 2), dma(nt * 2),
+        ],
+        compiler_params=pltpu.CompilerParams(
+            collective_id=0, has_side_effects=True, vmem_limit_bytes=48 << 20),
+        name="divergence_grad",
+    )(student_hidden, teacher_hidden, loss_weight.reshape(1, rows), student_head, teacher_head)
+    return grad, loss.reshape(())
 
 
 def divergence_terms(student_logits, teacher_logits, weights):
@@ -29,7 +374,7 @@
     return (divergence, scaled_gap)
 
 
-def shards(student_hidden, teacher_hidden, student_head, teacher_head, loss_weight):
+def plain_shards(student_hidden, teacher_hidden, student_head, teacher_head, loss_weight):
     student_block, teacher_block = (
         lax.all_gather(student_hidden, "voc", axis=1, tiled=True),
         lax.all_gather(teacher_hidden, "voc", axis=1, tiled=True),
@@ -75,8 +420,13 @@
         P("hid", "voc"),
         P("tok"),
     )
+    n, nt = mesh.shape["voc"], mesh.shape["tok"]
+    if n <= 4 and mesh.shape["hid"] == 2:
+        body = functools.partial(fused_shards, n, nt)
+    else:
+        body = plain_shards
     return jax.shard_map(
-        shards,
+        body,
         mesh=mesh,
         in_specs=placed,
         out_specs=(P("tok", ("hid", "voc")), P()),

time: 184 us -> 91.3 us (0.50)
  waiting for transfers between devices: 113 us -> 0 us
  Pallas kernels: 0 us -> 83.1 us
  blocking collectives: 34.3 us -> 0 us
  matrix products: 13.5 us -> 0 us
  between operations: 15.6 us -> 2.4 us
  other arithmetic: 6.6 us -> 0 us
  local copies, waits for them, and re-layouts: 0.08 us -> 5.53 us
    pallas_call x0 -> x1, Pallas kernels: none -> 83.1 us  [fused_shards(): pl.pallas_call(functools.partial(fused, n, nt), out_shape=(jax.ShapeDtype...]
    all_gather x2 -> x0, waiting for transfers between devices: 74.2 us -> none  [the longest x1 43.7 us: shards(): lax.all_gather(teacher_hidden, 'voc', axis=1, tiled=True)]
    reduce_scatter x2 -> x0, waiting for transfers between devices: 37.1 us -> none  [the longest x1 29.9 us: shards(): lax.psum_scatter(grad_terms, 'voc', scatter_dimension=1, tiled=True)]
    psum x2 -> x0, blocking collectives: 18.8 us -> none  [the longest x1 12.1 us: shards(): loss_total = lax.psum(jnp.sum(divergence), ('tok', 'hid'))]
    dot_general x3 -> x0, matrix products: 13.5 us -> none  [the longest x1 5.27 us: shards(): jnp.dot(teacher_block, teacher_head, preferred_element_type=jnp.float32)]
    pmax x1 -> x0, blocking collectives: 10.1 us -> none  [divergence_terms(): lax.pmax((jnp.max(student_logits, axis=1), jnp.max(teacher_logits, axis=1...]
    unnamed x2 -> x9, local copies, waits for them, and re-layouts: 0.01 us -> 5.53 us
    all_gather x1 -> x0, blocking collectives: 5.44 us -> none  [shards(): lax.all_gather(scaled_gap, 'hid', axis=0, tiled=True)]
  transfers between devices with their start and end apart: 4 -> 0, of which waited for: 4 -> 0; matrix products, arithmetic and copies ran while one was open for 2% -> 0% of each run, Pallas kernels for 0% -> 0%
where the time goes in v1:
time: 91.3 us; the launch traced here: 91 us
  Pallas kernels  83.1 us (91%)
  local copies, waits for them, and re-layouts  5.53 us (6%)
  between operations  2.4 us (3%)
    pallas_call x1, Pallas kernels, fused_shards(): pl.pallas_call(functools.partial(fused, n, nt), out_shape=(jax.ShapeDtype...  83.1 us
    unnamed x9, local copies, waits for them, and re-layouts  5.53 us

profile of v1, /device:TPU:1, one launch (start us, length us, event | category | flops | bytes accessed | tf_op | source)
XLA Modules:
  0.0 91.0 jit_solution(9367968060351728598)
XLA Ops:
  0.6 0.0 copy-start
  0.6 2.2 %copy-done = bf16[4096,512]{1,0:T(8,128)(2,1)S(1)} copy-done((bf16[4096,512]{1,0:T(8,128)(2,1)S(1)}, bf16[4096,512]{1,0:T(8,128)(2,1)}, u32[]{:S(2)}) %copy-start) | copy-done | bytes 4194328
  2.8 0.0 copy-start.1
  2.8 1.0 %copy-done.1 = bf16[128,2048]{1,0:T(8,128)(2,1)S(1)} copy-done((bf16[128,2048]{1,0:T(8,128)(2,1)S(1)}, bf16[128,2048]{1,0:T(8,128)(2,1)}, u32[]{:S(2)}) %copy-start.1) | copy-done | bytes 524312
  3.9 0.0 copy-start.2
  3.9 0.9 %copy-done.2 = bf16[128,1024]{1,0:T(8,128)(2,1)S(1)} copy-done((bf16[128,1024]{1,0:T(8,128)(2,1)S(1)}, bf16[128,1024]{1,0:T(8,128)(2,1)}, u32[]{:S(2)}) %copy-start.2) | copy-done | bytes 262168
  4.8 0.0 copy-start.3
  4.8 0.7 copy-done.3
  5.5 83.1 %divergence_grad.1 = (bf16[128,1024]{1,0:T(8,128)(2,1)S(1)}, f32[1,1]{1,0:T(1,128)}) custom-call(bf16[128,1024]{1,0:T(8,128)(2,1)S(1)} %copy-done.2, bf16[128,2048]{1,0:T(8,128)(2,1)S(1)} %copy-done.1, f32[1,128]{1,0:T(1,128)S(1)} %bitcast.2, bf16[4096,512]{1,0:T(8,128)(2,1)S(1)} %copy-done, bf16[8192,512]{1,0:T(8,128)(2,1)} %tw_hbm.1), custom_call_target="tpu_custom_call" | custom-call | tf_op jit(solution)/shard_map/divergence_grad/pallas_call | solution.py:318
  88.6 0.7 copy.9
Async XLA Ops:
  0.6 2.2 %copy-start = (bf16[4096,512]{1,0:T(8,128)(2,1)S(1)}, bf16[4096,512]{1,0:T(8,128)(2,1)}, u32[]{:S(2)}) copy-start(bf16[4096,512]{1,0:T(8,128)(2,1)} %sw_hbm.1) | copy-start | bytes 12582916
  2.8 1.0 %copy-start.1 = (bf16[128,2048]{1,0:T(8,128)(2,1)S(1)}, bf16[128,2048]{1,0:T(8,128)(2,1)}, u32[]{:S(2)}) copy-start(bf16[128,2048]{1,0:T(8,128)(2,1)} %y_ref.1) | copy-start | bytes 1572868
  3.9 0.9 %copy-start.2 = (bf16[128,1024]{1,0:T(8,128)(2,1)S(1)}, bf16[128,1024]{1,0:T(8,128)(2,1)}, u32[]{:S(2)}) copy-start(bf16[128,1024]{1,0:T(8,128)(2,1)} %x_ref.1) | copy-start | bytes 786436
  4.8 0.7 copy-start.3

commit v2 on v1

--- a/solution.py
+++ b/solution.py
@@ -12,8 +12,8 @@
 BF16 = jnp.bfloat16
 
 
-def fused(n, nt, x_ref, y_ref, w_ref, sw_hbm, tw_hbm, out, loss_out,
-          wf, tw, tg, sp, spx, ssum, srr, tacc, tpx, stat, gap, wcol, lossb, acc,
+def fused(n, nt, x_hbm, y_hbm, w_hbm, sw_hbm, tw_hbm, out, loss_out,
+          x_ref, y_ref, w_ref, wf, tw, tg, sp, spx, ssum, srr, tacc, tpx, stat, gap, wcol, lossb, acc,
           lc, wz_s, wz_r, wt_s, wt_r, th_s, th_r, px_s, px_r, rs_s, rs_r,
           st_s, st_r, gz_s, gz_r, gx_s, gx_r, ls_s, ls_r):
     z = lax.axis_index("voc")
@@ -44,6 +44,10 @@
 
     own_w = pltpu.make_async_copy(sw_hbm.at[pl.ds(pl.multiple_of(z * ks, ks), ks)], wf.at[z], lc.at[n])
     own_w.start()
+    ins = [pltpu.make_async_copy(a, b, lc.at[n + 1 + i])
+           for i, (a, b) in enumerate(((x_hbm, x_ref), (y_hbm, y_ref), (w_hbm, w_ref)))]
+    for c in ins:
+        c.start()
 
     def tw_copy(i):
         return pltpu.make_async_copy(tw_hbm.at[pl.ds(pl.multiple_of(i * kt, kt), kt)], tw.at[i], lc.at[i])
@@ -74,7 +78,7 @@
     def sides(d):
         return ((z - d, z - d >= 0), (z + d, z + d < n))
 
-    for d in range(1, n):
+    for d in range(n - 1, 0, -1):
         for j, ok in sides(d):
             @pl.when(ok)
             def _(j=j):
@@ -84,7 +88,7 @@
         return pl.ds(r * half, half)
 
     def own_y(r, side):
-        return rc(y_ref.at[piece(r)], tg.at[z, piece(r)], th_s.at[side, z, r], th_r.at[z, r],
+        return rc(y_hbm.at[piece(r)], tg.at[z, piece(r)], th_s.at[side, z, r], th_r.at[z, r],
                   {"voc": z + (1 if side else -1)})
 
     def relay_y(i, r, side):
@@ -101,9 +105,11 @@
     for k in range(n):
         tw_copy(zdev(k)).start()
 
+    for c in ins:
+        c.wait()
     wcol[...] = jnp.transpose(jnp.broadcast_to(w_ref[...], (rows, rows)))
 
-    for d in range(1, n):
+    for d in range(n - 1, 0, -1):
         for j, ok in sides(d):
             @pl.when(ok)
             def _(j=j):
@@ -153,42 +159,55 @@
             def _(i=i):
                 teacher_dot(tg.at[i], i, False)
 
-    def student(k):
-        j = zdev(k)
-        if k == 0:
+    def student(j, own):
+        if own:
             own_w.wait()
         else:
             for q in range(1, nt):
                 wt_in(j, lax.rem(t + q, nt)).wait_recv()
         sp[j] = jnp.dot(x_ref[...], wf[j], preferred_element_type=F32)
-        rc(sp.at[j, theirs], spx.at[j], px_s.at[j], px_r.at[j], partner).start()
-
-    def student_send(k):
-        j = zdev(k)
-        rc(sp.at[j, theirs], spx.at[j], px_s.at[j], px_r.at[j], partner).wait_recv()
+        swap = rc(sp.at[j, theirs], spx.at[j], px_s.at[j], px_r.at[j], partner)
+        swap.start()
+        swap.wait_recv()
         ssum[j] = sp[j, mine, :] + spx[j]
-        if k:
-            rc(ssum.at[j], srr.at[z], rs_s.at[j], rs_r.at[z], {"voc": j}).start()
-
-    student(0)
-    for d in range(1, n - 1):
-        take_y(d, True)
-    student_send(0)
-    for k in range(1, n):
-        student(k)
-        student_send(k)
+
+    def rs(side, j):
+        return rc(ssum.at[j], srr.at[side, j], rs_s.at[j], rs_r.at[side, j],
+                  {"voc": z + (1 if side else -1)})
+
+    def student_step(d):
+        for side, (j, ok) in enumerate(sides(d)):
+            @pl.when(ok)
+            def _(j=j, side=side):
+                student(j, False)
+
+                @pl.when(room[1 - side])
+                def _():
+                    rs(side, j).wait_recv()
+                    ssum[j] += srr[side, j]
+                rs(side, j).start()
+
+    take_y(1, False)
+    student_step(n - 1)
+    dot_y(1)
+    for d in range(n - 2, 0, -1):
+        if d == 1:
+            for e in range(2, n - 1):
+                take_y(e, True)
+        student_step(d)
+    student(z, True)
+    for side in range(2):
+        @pl.when(room[1 - side])
+        def _(side=side):
+            rs(side, z).wait_recv()
+            ssum[z] += srr[side, z]
+    sl = ssum[z]
+    ms = jnp.max(sl, axis=1, keepdims=True)
+    ss = jnp.sum(jnp.exp(sl - ms), axis=1, keepdims=True)
     take_y(n - 1, True)
 
     tx = rc(tacc.at[theirs], tpx, px_s.at[n], px_r.at[n], partner)
     tx.start()
-    sl = ssum[z]
-    for k in range(1, n):
-        j = zdev(k)
-        rc(srr.at[j], srr.at[j], rs_s.at[j], rs_r.at[j], {"voc": j}).wait_recv()
-        sl = sl + srr[j]
-    ssum[z] = sl
-    ms = jnp.max(sl, axis=1, keepdims=True)
-    ss = jnp.sum(jnp.exp(sl - ms), axis=1, keepdims=True)
     tx.wait_recv()
     tl = tacc[mine, :] + tpx[...]
     tpx[...] = tl
@@ -281,7 +300,7 @@
         wz(j).wait_send()
         for q in range(1, nt):
             wt(j, lax.rem(t + q, nt)).wait_send()
-        rc(ssum.at[j], srr.at[z], rs_s.at[j], rs_r.at[z], {"voc": j}).wait_send()
+        rc(ssum.at[j], srr.at[0, j], rs_s.at[j], rs_r.at[0, j], {"voc": j}).wait_send()
         stx(j, z).wait_send()
         gz(j, z).wait_send()
     for r in range(2):
@@ -318,16 +337,19 @@
     grad, loss = pl.pallas_call(
         functools.partial(fused, n, nt),
         out_shape=(jax.ShapeDtypeStruct((rows, ks), BF16), jax.ShapeDtypeStruct((1, 1), F32)),
-        in_specs=[whole, whole, whole, anywhere, anywhere],
+        in_specs=[anywhere] * 5,
         out_specs=(whole, pl.BlockSpec(memory_space=pltpu.SMEM)),
         scratch_shapes=[
+            vmem((rows, ks), BF16),
+            vmem((rows, kt), BF16),
+            vmem((1, rows), F32),
             vmem((n, ks, v), BF16),
             vmem((n, kt, v), BF16),
             vmem((n, rows, kt), BF16),
             vmem((n, rows, v), F32),
             vmem((n, half, v), F32),
             vmem((n, half, v), F32),
-            vmem((n, half, v), F32),
+            vmem((2, n, half, v), F32),
             vmem((rows, v), F32),
             vmem((half, v), F32),
             vmem((n, half, 128), F32),
@@ -335,10 +357,10 @@
             vmem((rows, rows), F32),
             vmem((nt * 2, 8, 128), F32),
             vmem((rows, ks), F32),
-            dma(n + 1),
+            dma(n + 4),
             dma(n), dma(n), dma(n, nt), dma(n, nt),
             dma(2, n, 2), dma(n, 2),
-            dma(n + 1), dma(n + 1), dma(n), dma(n),
+            dma(n + 1), dma(n + 1), dma(n), dma(2, n),
             dma(n), dma(n), dma(n), dma(n), dma(n), dma(n),
             dma(nt * 2), dma(nt * 2),
         ],
@@ -421,7 +443,7 @@
         P("tok"),
     )
     n, nt = mesh.shape["voc"], mesh.shape["tok"]
-    if n <= 4 and mesh.shape["hid"] == 2:
+    if 2 < n <= 4 and mesh.shape["hid"] == 2:
         body = functools.partial(fused_shards, n, nt)
     else:
         body = plain_shards

time: 91.3 us -> 87.4 us (0.957)
  Pallas kernels: 83.1 us -> 79.2 us
    pallas_call x1, Pallas kernels: 83.1 us -> 79.2 us  [fused_shards(): pl.pallas_call(functools.partial(fused, n, nt), out_shape=(jax.ShapeDtype...]
where the time goes in v2:
time: 87.4 us; the launch traced here: 87.1 us
  Pallas kernels  79.2 us (91%)
  local copies, waits for them, and re-layouts  5.53 us (6%)
  between operations  2.4 us (3%)
    pallas_call x1, Pallas kernels, fused_shards(): pl.pallas_call(functools.partial(fused, n, nt), out_shape=(jax.ShapeDtype...  79.2 us
    unnamed x9, local copies, waits for them, and re-layouts  5.53 us

profile of v2, /device:TPU:1, one launch (start us, length us, event | category | flops | bytes accessed | tf_op | source)
XLA Modules:
  0.0 87.1 jit_solution(11457107788325337873)
XLA Ops:
  0.6 0.0 copy-start
  0.6 2.2 %copy-done = bf16[4096,512]{1,0:T(8,128)(2,1)S(1)} copy-done((bf16[4096,512]{1,0:T(8,128)(2,1)S(1)}, bf16[4096,512]{1,0:T(8,128)(2,1)}, u32[]{:S(2)}) %copy-start) | copy-done | bytes 4194328
  2.8 0.0 copy-start.1
  2.8 1.0 %copy-done.1 = bf16[128,2048]{1,0:T(8,128)(2,1)S(1)} copy-done((bf16[128,2048]{1,0:T(8,128)(2,1)S(1)}, bf16[128,2048]{1,0:T(8,128)(2,1)}, u32[]{:S(2)}) %copy-start.1) | copy-done | bytes 524312
  3.9 0.0 copy-start.2
  3.9 0.9 %copy-done.2 = bf16[128,1024]{1,0:T(8,128)(2,1)S(1)} copy-done((bf16[128,1024]{1,0:T(8,128)(2,1)S(1)}, bf16[128,1024]{1,0:T(8,128)(2,1)}, u32[]{:S(2)}) %copy-start.2) | copy-done | bytes 262168
  4.8 0.0 copy-start.3
  4.8 0.7 copy-done.3
  5.5 79.2 %divergence_grad.1 = (bf16[128,1024]{1,0:T(8,128)(2,1)S(1)}, f32[1,1]{1,0:T(1,128)}) custom-call(bf16[128,1024]{1,0:T(8,128)(2,1)S(1)} %copy-done.2, bf16[128,2048]{1,0:T(8,128)(2,1)S(1)} %copy-done.1, f32[1,128]{1,0:T(1,128)S(1)} %bitcast.2, bf16[4096,512]{1,0:T(8,128)(2,1)S(1)} %copy-done, bf16[8192,512]{1,0:T(8,128)(2,1)} %tw_hbm.1), custom_call_target="tpu_custom_call" | custom-call | tf_op jit(solution)/shard_map/divergence_grad/pallas_call | solution.py:337
  84.7 0.7 copy.9
Async XLA Ops:
  0.6 2.2 %copy-start = (bf16[4096,512]{1,0:T(8,128)(2,1)S(1)}, bf16[4096,512]{1,0:T(8,128)(2,1)}, u32[]{:S(2)}) copy-start(bf16[4096,512]{1,0:T(8,128)(2,1)} %sw_hbm.1) | copy-start | bytes 12582916
  2.8 1.0 %copy-start.1 = (bf16[128,2048]{1,0:T(8,128)(2,1)S(1)}, bf16[128,2048]{1,0:T(8,128)(2,1)}, u32[]{:S(2)}) copy-start(bf16[128,2048]{1,0:T(8,128)(2,1)} %y_hbm.1) | copy-start | bytes 1572868
  3.9 0.9 %copy-start.2 = (bf16[128,1024]{1,0:T(8,128)(2,1)S(1)}, bf16[128,1024]{1,0:T(8,128)(2,1)}, u32[]{:S(2)}) copy-start(bf16[128,1024]{1,0:T(8,128)(2,1)} %x_hbm.1) | copy-start | bytes 786436
  4.8 0.7 copy-start.3

commit v3 on v2

--- a/solution.py
+++ b/solution.py
@@ -365,7 +365,7 @@
             dma(nt * 2), dma(nt * 2),
         ],
         compiler_params=pltpu.CompilerParams(
-            collective_id=0, has_side_effects=True, vmem_limit_bytes=48 << 20),
+            collective_id=0, has_side_effects=True, vmem_limit_bytes=60 << 20),
         name="divergence_grad",
     )(student_hidden, teacher_hidden, loss_weight.reshape(1, rows), student_head, teacher_head)
     return grad, loss.reshape(())

time: 87.4 us -> 83.7 us (0.958)
  local copies, waits for them, and re-layouts: 5.53 us -> 1.67 us
    unnamed x9 -> x1, local copies, waits for them, and re-layouts: 5.53 us -> 1.67 us
where the time goes in v3:
time: 83.7 us; the launch traced here: 83.6 us
  Pallas kernels  79.5 us (95%)
  between operations  2.4 us (3%)
  local copies, waits for them, and re-layouts  1.67 us (2%)
    pallas_call x1, Pallas kernels, fused_shards(): pl.pallas_call(functools.partial(fused, n, nt), out_shape=(jax.ShapeDtype...  79.5 us

profile of v3, /device:TPU:1, one launch (start us, length us, event | category | flops | bytes accessed | tf_op | source)
XLA Modules:
  0.0 83.6 jit_solution(9740654130142973811)
XLA Ops:
  0.6 79.5 %divergence_grad.1 = (bf16[128,1024]{1,0:T(8,128)(2,1)}, f32[1,1]{1,0:T(1,128)}) custom-call(bf16[128,1024]{1,0:T(8,128)(2,1)} %x_hbm.1, bf16[128,2048]{1,0:T(8,128)(2,1)} %y_hbm.1, f32[1,128]{1,0:T(1,128)} %bitcast.2, bf16[4096,512]{1,0:T(8,128)(2,1)} %sw_hbm.1, bf16[8192,512]{1,0:T(8,128)(2,1)} %tw_hbm.1), custom_call_target="tpu_custom_call" | custom-call | tf_op jit(solution)/shard_map/divergence_grad/pallas_call | solution.py:337
  80.1 1.7 %copy.9 = bf16[128,1024]{1,0:T(8,128)(2,1)} copy(bf16[128,1024]{1,0:T(8,128)(2,1)} %get-tuple-element.8) | data formatting | bytes 524288

commit v4 on v3

--- a/solution.py
+++ b/solution.py
@@ -69,11 +69,25 @@
     def wz_in(j):
         return rc(wf.at[j, part(t)], wf.at[j, part(t)], wz_s.at[j], wz_r.at[j], {"voc": j})
 
-    def wt(j, dst_t):
-        return rc(wf.at[j, part(t)], wf.at[j, part(t)], wt_s.at[j, dst_t], wt_r.at[j, t], {"tok": dst_t})
-
-    def wt_in(j, src_t):
-        return rc(wf.at[j, part(src_t)], wf.at[j, part(src_t)], wt_s.at[j, src_t], wt_r.at[j, src_t], {"tok": src_t})
+    side_x = t + 1 - 2 * lax.rem(t, 2)
+    side_y = lax.rem(t + 2, 4)
+    opposite = 3 - t
+    near = (side_x, side_y)
+
+    def wt(j, o, p, to):
+        rows_of = pl.ds(pl.multiple_of(o * quarter + p * (quarter // 2), quarter // 2), quarter // 2)
+        return rc(wf.at[j, rows_of], wf.at[j, rows_of], wt_s.at[to, j, o, p], wt_r.at[j, o, p],
+                  {"tok": near[to]})
+
+    def spread(j):
+        for i in range(2):
+            wt(j, t, i, 0).start()
+            wt(j, t, 1 - i, 1).start()
+
+    def pass_on(j):
+        for p in range(2):
+            wt(j, near[p], p, 1 - p).wait_recv()
+            wt(j, near[p], p, 1 - p).start()
 
     def sides(d):
         return ((z - d, z - d >= 0), (z + d, z + d < n))
@@ -114,8 +128,7 @@
             @pl.when(ok)
             def _(j=j):
                 wz_in(j).wait_recv()
-                for q in range(1, nt):
-                    wt(j, lax.rem(t + q, nt)).start()
+                spread(j)
 
     def teacher_dot(src, i, first):
         tw_copy(i).wait()
@@ -163,8 +176,10 @@
         if own:
             own_w.wait()
         else:
-            for q in range(1, nt):
-                wt_in(j, lax.rem(t + q, nt)).wait_recv()
+            wt(j, side_x, 1, 0).wait_recv()
+            wt(j, side_y, 0, 0).wait_recv()
+            wt(j, opposite, 0, 0).wait_recv()
+            wt(j, opposite, 1, 0).wait_recv()
         sp[j] = jnp.dot(x_ref[...], wf[j], preferred_element_type=F32)
         swap = rc(sp.at[j, theirs], spx.at[j], px_s.at[j], px_r.at[j], partner)
         swap.start()
@@ -188,6 +203,11 @@
                 rs(side, j).start()
 
     take_y(1, False)
+    for d in range(n - 1, 0, -1):
+        for j, ok in sides(d):
+            @pl.when(ok)
+            def _(j=j):
+                pass_on(j)
     student_step(n - 1)
     dot_y(1)
     for d in range(n - 2, 0, -1):
@@ -216,8 +236,9 @@
     st = jnp.sum(et, axis=1, keepdims=True)
     cr = jnp.sum(et * (tl - sl), axis=1, keepdims=True)
     lane = lax.broadcasted_iota(jnp.int32, (half, 128), 1)
-    stat[z] = jnp.where(lane == 0, ms, jnp.where(lane == 1, mt, jnp.where(
+    cols = jnp.where(lane == 0, ms, jnp.where(lane == 1, mt, jnp.where(
         lane == 2, ss, jnp.where(lane == 3, st, cr))))
+    stat[z] = jnp.transpose(jnp.concatenate([cols] * (128 // half), axis=0))[:8]
 
     def stx(j, src):
         return rc(stat.at[src], stat.at[src], st_s.at[j], st_r.at[src], {"voc": j})
@@ -230,20 +251,23 @@
     top = parts[0]
     for p in parts[1:]:
         top = jnp.maximum(top, p)
-    big_s, big_t = top[:, 0:1], top[:, 1:2]
+    big_s, big_t = top[0:1], top[1:2]
     tot_s = jnp.zeros_like(big_s)
     tot_t = jnp.zeros_like(big_s)
     cross = jnp.zeros_like(big_s)
     for p in parts:
-        es = jnp.exp(p[:, 0:1] - big_s)
-        ets = jnp.exp(p[:, 1:2] - big_t)
-        tot_s = tot_s + p[:, 2:3] * es
-        tot_t = tot_t + p[:, 3:4] * ets
-        cross = cross + p[:, 4:5] * ets
+        es = jnp.exp(p[0:1] - big_s)
+        ets = jnp.exp(p[1:2] - big_t)
+        tot_s = tot_s + p[2:3] * es
+        tot_t = tot_t + p[3:4] * ets
+        cross = cross + p[4:5] * ets
     lse_s = big_s + jnp.log(tot_s)
     lse_t = big_t + jnp.log(tot_t)
     scale = wcol[mine, :][:, 0:1]
-    gap[z, mine, :] = (scale * (jnp.exp(ssum[z] - lse_s) - jnp.exp(tpx[...] - lse_t))).astype(BF16)
+    sub = lax.broadcasted_iota(jnp.int32, (128, 128), 0)
+    back = jnp.transpose(jnp.where(sub == 0, lse_s, lse_t))[:half]
+    col_s, col_t = back[:, 0:1], back[:, 1:2]
+    gap[z, mine, :] = (scale * (jnp.exp(ssum[z] - col_s) - jnp.exp(tpx[...] - col_t))).astype(BF16)
 
     def gz(j, src):
         return rc(gap.at[src, mine], gap.at[src, mine], gz_s.at[j], gz_r.at[src], {"voc": j})
@@ -259,7 +283,8 @@
     gx(z, mine).start()
 
     div = cross / tot_t - lse_t + lse_s
-    lossb[me] = jnp.broadcast_to(jnp.sum(div, axis=0, keepdims=True), (8, 128))
+    first = lax.broadcasted_iota(jnp.int32, div.shape, 1) < half
+    lossb[me] = jnp.broadcast_to(jnp.sum(jnp.where(first, div, 0.0), axis=1, keepdims=True), (8, 128))
 
     def ls(a, b, src):
         return rc(lossb.at[src], lossb.at[src], ls_s.at[a * 2 + b], ls_r.at[src], {"tok": a, "hid": b})
@@ -298,8 +323,10 @@
     for k in range(1, n):
         j = zdev(k)
         wz(j).wait_send()
-        for q in range(1, nt):
-            wt(j, lax.rem(t + q, nt)).wait_send()
+        for p in range(2):
+            wt(j, t, p, 0).wait_send()
+            wt(j, t, p, 1).wait_send()
+            wt(j, near[p], p, 1 - p).wait_send()
         rc(ssum.at[j], srr.at[0, j], rs_s.at[j], rs_r.at[0, j], {"voc": j}).wait_send()
         stx(j, z).wait_send()
         gz(j, z).wait_send()
@@ -352,13 +379,13 @@
             vmem((2, n, half, v), F32),
             vmem((rows, v), F32),
             vmem((half, v), F32),
-            vmem((n, half, 128), F32),
+            vmem((n, 8, 128), F32),
             vmem((n, rows, v), BF16),
             vmem((rows, rows), F32),
             vmem((nt * 2, 8, 128), F32),
             vmem((rows, ks), F32),
             dma(n + 4),
-            dma(n), dma(n), dma(n, nt), dma(n, nt),
+            dma(n), dma(n), dma(2, n, nt, 2), dma(n, nt, 2),
             dma(2, n, 2), dma(n, 2),
             dma(n + 1), dma(n + 1), dma(n), dma(2, n),
             dma(n), dma(n), dma(n), dma(n), dma(n), dma(n),
@@ -443,7 +470,7 @@
         P("tok"),
     )
     n, nt = mesh.shape["voc"], mesh.shape["tok"]
-    if 2 < n <= 4 and mesh.shape["hid"] == 2:
+    if 2 < n <= 4 and nt == 4 and mesh.shape["hid"] == 2:
         body = functools.partial(fused_shards, n, nt)
     else:
         body = plain_shards

time: 83.7 us -> 85.2 us (1.018)
  Pallas kernels: 79.5 us -> 80.9 us
    pallas_call x1, Pallas kernels: 79.5 us -> 80.9 us  [fused_shards(): pl.pallas_call(functools.partial(fused, n, nt), out_shape=(jax.ShapeDtype...]
where the time goes in v4:
time: 85.2 us; the launch traced here: 85 us
  Pallas kernels  80.9 us (95%)
  between operations  2.4 us (3%)
  local copies, waits for them, and re-layouts  1.67 us (2%)
    pallas_call x1, Pallas kernels, fused_shards(): pl.pallas_call(functools.partial(fused, n, nt), out_shape=(jax.ShapeDtype...  80.9 us

profile of v4, /device:TPU:1, one launch (start us, length us, event | category | flops | bytes accessed | tf_op | source)
XLA Modules:
  0.0 85.0 jit_solution(11389802565946803388)
XLA Ops:
  0.6 80.9 %divergence_grad.1 = (bf16[128,1024]{1,0:T(8,128)(2,1)}, f32[1,1]{1,0:T(1,128)}) custom-call(bf16[128,1024]{1,0:T(8,128)(2,1)} %x_hbm.1, bf16[128,2048]{1,0:T(8,128)(2,1)} %y_hbm.1, f32[1,128]{1,0:T(1,128)} %bitcast.2, bf16[4096,512]{1,0:T(8,128)(2,1)} %sw_hbm.1, bf16[8192,512]{1,0:T(8,128)(2,1)} %tw_hbm.1), custom_call_target="tpu_custom_call" | custom-call | tf_op jit(solution)/shard_map/divergence_grad/pallas_call | solution.py:364
  81.6 1.7 %copy.9 = bf16[128,1024]{1,0:T(8,128)(2,1)} copy(bf16[128,1024]{1,0:T(8,128)(2,1)} %get-tuple-element.8) | data formatting | bytes 524288

commit v5 on v3

--- a/solution.py
+++ b/solution.py
@@ -216,8 +216,9 @@
     st = jnp.sum(et, axis=1, keepdims=True)
     cr = jnp.sum(et * (tl - sl), axis=1, keepdims=True)
     lane = lax.broadcasted_iota(jnp.int32, (half, 128), 1)
-    stat[z] = jnp.where(lane == 0, ms, jnp.where(lane == 1, mt, jnp.where(
+    cols = jnp.where(lane == 0, ms, jnp.where(lane == 1, mt, jnp.where(
         lane == 2, ss, jnp.where(lane == 3, st, cr))))
+    stat[z] = jnp.transpose(jnp.concatenate([cols] * (128 // half), axis=0))[:8]
 
     def stx(j, src):
         return rc(stat.at[src], stat.at[src], st_s.at[j], st_r.at[src], {"voc": j})
@@ -230,20 +231,23 @@
     top = parts[0]
     for p in parts[1:]:
         top = jnp.maximum(top, p)
-    big_s, big_t = top[:, 0:1], top[:, 1:2]
+    big_s, big_t = top[0:1], top[1:2]
     tot_s = jnp.zeros_like(big_s)
     tot_t = jnp.zeros_like(big_s)
     cross = jnp.zeros_like(big_s)
     for p in parts:
-        es = jnp.exp(p[:, 0:1] - big_s)
-        ets = jnp.exp(p[:, 1:2] - big_t)
-        tot_s = tot_s + p[:, 2:3] * es
-        tot_t = tot_t + p[:, 3:4] * ets
-        cross = cross + p[:, 4:5] * ets
+        es = jnp.exp(p[0:1] - big_s)
+        ets = jnp.exp(p[1:2] - big_t)
+        tot_s = tot_s + p[2:3] * es
+        tot_t = tot_t + p[3:4] * ets
+        cross = cross + p[4:5] * ets
     lse_s = big_s + jnp.log(tot_s)
     lse_t = big_t + jnp.log(tot_t)
     scale = wcol[mine, :][:, 0:1]
-    gap[z, mine, :] = (scale * (jnp.exp(ssum[z] - lse_s) - jnp.exp(tpx[...] - lse_t))).astype(BF16)
+    sub = lax.broadcasted_iota(jnp.int32, (128, 128), 0)
+    back = jnp.transpose(jnp.where(sub == 0, lse_s, lse_t))[:half]
+    col_s, col_t = back[:, 0:1], back[:, 1:2]
+    gap[z, mine, :] = (scale * (jnp.exp(ssum[z] - col_s) - jnp.exp(tpx[...] - col_t))).astype(BF16)
 
     def gz(j, src):
         return rc(gap.at[src, mine], gap.at[src, mine], gz_s.at[j], gz_r.at[src], {"voc": j})
@@ -259,7 +263,8 @@
     gx(z, mine).start()
 
     div = cross / tot_t - lse_t + lse_s
-    lossb[me] = jnp.broadcast_to(jnp.sum(div, axis=0, keepdims=True), (8, 128))
+    first = lax.broadcasted_iota(jnp.int32, div.shape, 1) < half
+    lossb[me] = jnp.broadcast_to(jnp.sum(jnp.where(first, div, 0.0), axis=1, keepdims=True), (8, 128))
 
     def ls(a, b, src):
         return rc(lossb.at[src], lossb.at[src], ls_s.at[a * 2 + b], ls_r.at[src], {"tok": a, "hid": b})
@@ -352,7 +357,7 @@
             vmem((2, n, half, v), F32),
             vmem((rows, v), F32),
             vmem((half, v), F32),
-            vmem((n, half, 128), F32),
+            vmem((n, 8, 128), F32),
             vmem((n, rows, v), BF16),
             vmem((rows, rows), F32),
             vmem((nt * 2, 8, 128), F32),

time: 83.7 us -> 82.9 us (level)
  no operation moved by 1% of the time
where the time goes in v5:
time: 82.9 us; the launch traced here: 82.7 us
  Pallas kernels  78.7 us (95%)
  between operations  2.4 us (3%)
  local copies, waits for them, and re-layouts  1.67 us (2%)
    pallas_call x1, Pallas kernels, fused_shards(): pl.pallas_call(functools.partial(fused, n, nt), out_shape=(jax.ShapeDtype...  78.7 us
    unnamed x1, local copies, waits for them, and re-layouts  1.67 us

profile of v5, /device:TPU:1, one launch (start us, length us, event | category | flops | bytes accessed | tf_op | source)
XLA Modules:
  0.0 82.7 jit_solution(603979957513369897)
XLA Ops:
  0.6 78.7 %divergence_grad.1 = (bf16[128,1024]{1,0:T(8,128)(2,1)}, f32[1,1]{1,0:T(1,128)}) custom-call(bf16[128,1024]{1,0:T(8,128)(2,1)} %x_hbm.1, bf16[128,2048]{1,0:T(8,128)(2,1)} %y_hbm.1, f32[1,128]{1,0:T(1,128)} %bitcast.2, bf16[4096,512]{1,0:T(8,128)(2,1)} %sw_hbm.1, bf16[8192,512]{1,0:T(8,128)(2,1)} %tw_hbm.1), custom_call_target="tpu_custom_call" | custom-call | tf_op jit(solution)/shard_map/divergence_grad/pallas_call | solution.py:342
  79.3 1.7 %copy.9 = bf16[128,1024]{1,0:T(8,128)(2,1)} copy(bf16[128,1024]{1,0:T(8,128)(2,1)} %get-tuple-element.8) | data formatting | bytes 524288
